TPU v7x, 32 devices: a whole 2x2x4 slice. The times are simulated.
32 devices in a mesh: wide: 4 (over y, x), narrow: 8 (over z, core).
Axes of the slice: x: 2, y: 2, z: 4, core: 2. Of those that a mesh axis runs over, the one named last changes fastest.
Arguments:
- tokens: bfloat16 [4096, 4096], P('narrow'), may hold values from -6 to 6
- norm_gain: float32 [4096], replicated, may hold values from 0.1 to 1.9
- coded: bfloat16 [4096, 14336], P('narrow', 'wide'), may hold values from -0.09375 to 0.09375
- block_codes: int32 [32, 112], P('narrow', 'wide'), may hold values from 0 to 15
- grid: float32 [16], replicated, may hold values from 0.5 to 2
- cotangent: bfloat16 [4096, 14336], P('narrow', 'wide'), may hold values from -6 to 6
Outputs:
- activated: bfloat16 [4096, 14336], P('narrow', 'wide')
- weight_grad: float32 [4096, 14336], P('narrow', 'wide')
- input_grad: bfloat16 [4096, 4096], P('narrow', 'wide')
All inputs are finite; a program needn't handle non-finite values.
Results may differ from a plain program's by a relative error of at most 0.017.
Values may be sent and summed in bfloat16 or wider, within the bound.
No kernel may reach another device: no remote copies, remote signals or barrier semaphores. Data moves between devices by JAX's collectives and lax.ppermute only.
A program may use at most 128 MiB of HBM per device.

v0:
```python
import jax
import jax.numpy as jnp
from jax import lax
from jax.sharding import PartitionSpec as P

BLOCK = 128


def hadamard(size):
    index = jnp.arange(size, dtype=jnp.int32)
    parity = jnp.zeros((size, size), jnp.int32)
    for level in range(size.bit_length() - 1):
        stride = 2**level
        parity = parity + index[:, None] // stride % 2 * (index[None, :] // stride % 2)
    return (1 - 2 * (parity % 2)).astype(jnp.bfloat16)


def decode(coded, block_codes, grid):
    nrows, ncols = coded.shape
    rotation = hadamard(BLOCK)
    onehot = (
        block_codes[:, :, None] == jnp.arange(grid.shape[0], dtype=jnp.int32)[None, None, :]
    ).astype(jnp.float32)
    block_scale = jnp.sum(onehot * grid[None, None, :], axis=-1) / jnp.sqrt(jnp.float32(BLOCK))
    blocks = coded.reshape(nrows // BLOCK, BLOCK, ncols // BLOCK, BLOCK)

    def one_row(pair):
        piece, scales = pair
        turned = jnp.einsum("ikj,jl->ikl", piece, rotation, preferred_element_type=jnp.float32)
        return (turned * scales[None, :, None]).reshape(BLOCK, ncols).astype(jnp.bfloat16)

    return lax.map(one_row, (blocks, block_scale)).reshape(nrows, ncols)


def per_device(tokens, norm_gain, coded, block_codes, grid, cotangent):
    weight = lax.all_gather(decode(coded, block_codes, grid), "narrow", axis=0, tiled=True)
    inputs = tokens.astype(jnp.float32)
    inv_rms = lax.rsqrt(jnp.mean(inputs * inputs, axis=-1, keepdims=True) + 1e-05)
    normed = (inputs * inv_rms * norm_gain[None, :]).astype(jnp.bfloat16)
    preact = jnp.dot(normed, weight, preferred_element_type=jnp.float32)
    sig = jax.nn.sigmoid(preact)
    activated = (preact * sig).astype(jnp.bfloat16)
    pre_grad = (cotangent.astype(jnp.float32) * sig * (1.0 + preact * (1.0 - sig))).astype(
        jnp.bfloat16
    )
    weight_grad = lax.psum_scatter(
        lax.dot_general(
            normed, pre_grad, (((0,), (0,)), ((), ())), preferred_element_type=jnp.float32
        ).astype(jnp.bfloat16),
        "narrow",
        scatter_dimension=0,
        tiled=True,
    ).astype(jnp.float32)
    partial_value = lax.dot_general(
        pre_grad, weight, (((1,), (1,)), ((), ())), preferred_element_type=jnp.float32
    )
    share = inputs.shape[1] // lax.axis_size("wide")
    offset = lax.axis_index("wide") * share
    normed_grad = lax.psum(partial_value.astype(jnp.bfloat16), "wide").astype(jnp.float32)
    scaled_grad = normed_grad * norm_gain[None, :]
    row_dot = jnp.mean(scaled_grad * inputs, axis=-1, keepdims=True)
    full_grad = inv_rms * scaled_grad - inputs * inv_rms**3 * row_dot
    input_grad = lax.dynamic_slice_in_dim(full_grad, offset, share, 1).astype(jnp.bfloat16)
    return (activated, weight_grad, input_grad)


def solution(mesh):
    placed = (
        P("narrow", None),
        P(),
        P("narrow", "wide"),
        P("narrow", "wide"),
        P(),
        P("narrow", "wide"),
    )
    return jax.shard_map(
        per_device,
        mesh=mesh,
        in_specs=placed,
        out_specs=(P("narrow", "wide"), P("narrow", "wide"), P("narrow", "wide")),
        check_vma=False,
    )
```

profile of v0, /device:TPU:0, one launch (start us, length us, event | category | flops | bytes accessed | tf_op | source)
XLA Modules:
  0.0 751.2 jit_solution(8268245309656410113)
XLA Ops:
  7.2 0.0 all-gather.2.cloned.1.call-start
  7.3 0.0 copy-start.1
  7.3 0.0 copy-start.2
  7.3 7.1 reshape.708
  14.3 5.4 copy.13
  19.7 0.0 copy-done.1
  19.7 0.0 copy-done.2
  19.7 0.1 select_reduce_fusion
  19.8 13.0 %while.11 = (s32[]{:T(128)}, bf16[4,128,3584]{2,1,0:T(8,128)(2,1)}, bf16[4,128,28,128]{3,1,2,0:T(8,128)(2,1)}, f32[4,28]{1,0:T(4,128)S(1)}, s32[128]{0:T(128)S(1...) while((s32[]{:T(128)}, bf16[4,128,3584]{2,1,0:T(8,128)(2,1)}, ...), condition=%wide.region_3.4_spmd.clone, body=%wide.region_2.3_spmd.clone.sunk | while | flops 118800384 | bytes 5514073 | solution.py:32
  19.9 1.7 multiply_convert_fusion.9
  21.6 0.5 copy.20
  22.1 1.0 constant_dynamic-update-slice_fusion.2
  23.1 1.7 multiply_convert_fusion.9
  24.8 0.5 copy.20
  25.4 1.0 constant_dynamic-update-slice_fusion.2
  26.4 1.7 multiply_convert_fusion.9
  28.1 0.5 copy.20
  28.6 1.0 constant_dynamic-update-slice_fusion.2
  29.6 1.7 multiply_convert_fusion.9
  31.3 0.5 copy.20
  31.9 1.0 constant_dynamic-update-slice_fusion.2
  32.8 0.0 copy-start
  32.8 0.0 all-gather.2.cloned.1.call-update
  32.9 0.2 all-reduce.2.cloned.1.call-start
  33.1 3.1 multiply_reduce_fusion.1
  36.2 253.8 %all-gather.2.cloned.1.call-done = bf16[4096,3584]{1,0:T(8,128)(2,1)} async-done(((bf16[512,3584]{1,0:T(8,128)(2,1)}), bf16[4096,3584]{1,0:T(8,128)(2,1)}) %all-gather.2.cloned.1.call-update) | async-done | bytes 29360144 | tf_op jit(solution)/shard_map/all_gather | solution.py:36
  290.0 0.0 copy-done
  290.0 25.1 %multiply_convert_fusion.3 = (bf16[512,3584]{1,0:T(8,128)(2,1)}, f32[512,3584]{1,0:T(8,128)}) fusion(bf16[4096,3584]{1,0:T(8,128)(2,1)} %all-gather.2.cloned.1.call-done, bf16[512,4096]{1,0:T(8,128)(2,1)} %param.8, f32[4096]{0:T(1024)S(1)} %copy-done, f32[512]{0:T(512)S(1)} %get-tuple-element.109), kind=kOutput, calls=%fused_computation.41 | convolution fusion | flops 15049949184 | bytes 44582912 | tf_op jit(solution)/shard_map/dot_general | solution.py:40
  315.1 32.6 %convolution_convert_fusion.1 = bf16[512,4096]{1,0:T(8,128)(2,1)} fusion(bf16[4096,3584]{1,0:T(8,128)(2,1)} %all-gather.2.cloned.1.call-done, f32[512,3584]{1,0:T(8,128)} %get-tuple-element.111, bf16[512,3584]{1,0:T(8,128)(2,1)} %param.13), kind=kOutput, calls=%fused_computation.43 | convolution fusion | flops 15052832768 | bytes 44564480 | tf_op jit(solution)/shard_map/dot_general | solution.py:54
  347.7 0.0 all-reduce.2.cloned.1.call-update
  347.7 0.3 reduce-scatter.2.cloned.1.call-start
  348.0 25.9 %convolution_convert_fusion = bf16[4096,3584]{1,0:T(8,128)(2,1)} fusion(bf16[512,4096]{1,0:T(8,128)(2,1)} %param.8, f32[4096]{0:T(1024)S(1)} %copy-done, f32[512]{0:T(512)S(1)} %get-tuple-element.109, f32[512,3584]{1,0:T(8,128)} %get-tuple-element.111, bf16[512,3584]{1,0:T(8,128)(2,1)} %param.13), kind=kOutput, calls=%fused_computation.35 | convolution fusion | flops 15073804288 | bytes 44582912 | tf_op jit(solution)/shard_map/dot_general | solution.py:47
  373.9 0.0 reduce-scatter.2.cloned.1.call-update
  374.0 6.7 convert_element_type.47
  380.7 69.0 %all-reduce.2.cloned.1.call-done = bf16[512,4096]{1,0:T(8,128)(2,1)} async-done(((bf16[512,4096]{1,0:T(8,128)(2,1)}), bf16[512,4096]{1,0:T(8,128)(2,1)}) %all-reduce.2.cloned.1.call-update) | async-done | bytes 4194320 | tf_op jit(solution)/shard_map/psum | solution.py:59
  449.7 4.9 multiply_reduce_fusion
  454.6 3.0 fusion.32
  457.5 281.1 %reduce-scatter.2.cloned.1.call-done = bf16[512,3584]{1,0:T(8,128)(2,1)} async-done(((bf16[4096,3584]{1,0:T(8,128)(2,1)}), bf16[512,3584]{1,0:T(8,128)(2,1)}) %reduce-scatter.2.cloned.1.call-update) | async-done | bytes 3670032 | tf_op jit(solution)/shard_map/reduce_scatter | solution.py:46
  738.6 6.0 convert_element_type.54
  (12 shorter events, 0.1 us)
Async XLA Ops:
  7.2 282.8 %all-gather.2.cloned.1.call-start = ((), (), s32[]{:S(2)}) async-start(), calls=%async_computation.1 | async-start | bytes 33030144 | tf_op jit(solution)/shard_map/all_gather | solution.py:36
  7.3 12.5 %copy-start.1 = (s32[4,28]{1,0:T(4,128)S(1)}, s32[4,28]{1,0:T(4,128)}, u32[]{:S(2)}) copy-start(s32[4,28]{1,0:T(4,128)} %param.11) | copy-start | bytes 1348
  7.3 12.5 %copy-start.2 = (f32[16]{0:T(128)S(1)}, f32[16]{0:T(128)}, u32[]{:S(2)}) copy-start(f32[16]{0:T(128)} %param.12) | copy-start | bytes 196
  32.8 257.1 %copy-start = (f32[4096]{0:T(1024)S(1)}, f32[4096]{0:T(1024)}, u32[]{:S(2)}) copy-start(f32[4096]{0:T(1024)} %param.9) | copy-start | bytes 49156
  32.9 416.8 %all-reduce.2.cloned.1.call-start = ((), (), s32[]{:S(2)}) async-start(), calls=%async_computation.3 | async-start | bytes 8388608 | tf_op jit(solution)/shard_map/psum | solution.py:59
  347.7 390.9 %reduce-scatter.2.cloned.1.call-start = ((), (), s32[]{:S(2)}) async-start(), calls=%async_computation.2 | async-start | bytes 33030144 | tf_op jit(solution)/shard_map/reduce_scatter | solution.py:46
Sparse Core Ops, SparseCore 0:
  33.0 256.9 all-gather.1
  347.8 101.7 all-reduce.1
  452.0 286.5 reduce-scatter.1
where the time goes:
time: 752 us; the launch traced here: 751 us
  waiting for transfers between devices  604 us (80%)
  matrix products  90.5 us (12%)
  other arithmetic  23.8 us (3%)
  local copies, waits for them, and re-layouts  18.5 us (2%)
  between operations  13.8 us (2%)
    reduce_scatter x1, waiting for transfers between devices, per_device(): lax.psum_scatter(lax.dot_general(normed, pre_grad, (((0,), (0,)), ((), ()...  281 us
    all_gather x1, waiting for transfers between devices, per_device(): lax.all_gather(decode(coded, block_codes, grid), 'narrow', axis=0, tiled=...  254 us
    psum x1, waiting for transfers between devices, per_device(): lax.psum(partial_value.astype(jnp.bfloat16), 'wide').astype(jnp.float32)  69 us
    dot_general x1, matrix products, per_device(): lax.dot_general(pre_grad, weight, (((1,), (1,)), ((), ())), preferred_ele...  32.6 us
    dot_general x1, matrix products, per_device(): lax.dot_general(normed, pre_grad, (((0,), (0,)), ((), ())), preferred_ele...  25.9 us
    dot_general x1, matrix products, per_device(): preact = jnp.dot(normed, weight, preferred_element_type=jnp.float32)  25.1 us
  transfers between devices with their start and end apart: 3, of which 3 were waited for; matrix products, arithmetic and copies ran while one was open for 6% of the time, Pallas kernels for 0%

commit v1 on v0

v1 whole, which is shorter than its diff:
```python
import jax
import jax.numpy as jnp
from jax import lax
from jax.sharding import PartitionSpec as P


BLOCK = 128
CHUNKS = 4
DEPTH = 2


def hadamard(size):
    index = jnp.arange(size, dtype=jnp.int32)
    parity = jnp.zeros((size, size), jnp.int32)
    for level in range(size.bit_length() - 1):
        stride = 2**level
        parity = parity + index[:, None] // stride % 2 * (index[None, :] // stride % 2)
    return (1 - 2 * (parity % 2)).astype(jnp.bfloat16)


def turn(ncols):
    nblk = ncols // BLOCK
    tiled = jnp.tile(hadamard(BLOCK), (nblk, nblk))
    where = jnp.arange(ncols, dtype=jnp.int32) // BLOCK
    return jnp.where(where[:, None] == where[None, :], tiled, jnp.zeros_like(tiled))


def decode(coded, scale):
    _, cols = coded.shape
    turned = jnp.dot(coded, turn(cols), preferred_element_type=jnp.float32)
    wide_scale = jnp.repeat(jnp.repeat(scale, BLOCK, axis=0), BLOCK, axis=1)
    return (turned * wide_scale).astype(jnp.bfloat16)


def cuts(blocks, pieces):
    pieces = min(pieces, blocks)
    edges = [(blocks * i + pieces - 1) // pieces for i in range(pieces + 1)]
    return [(lo * BLOCK, hi * BLOCK) for lo, hi in zip(edges, edges[1:])]


def plan(n):
    out = [("share", 0), ("weight", 0), ("norm", 0), ("near", 0), ("far", 0)]
    out += [("weight", k) for k in range(1, min(DEPTH, n))]
    out += [("cot", 0), ("cross", 0)]
    for k in range(n):
        out.append(("fwd", k))
        if k + DEPTH < n:
            out.append(("weight", k + DEPTH))
        out.append(("own", k))
        if k >= 1:
            out.append(("epi", k - 1))
        if k >= 2:
            out.append(("bwd", k - 2))
    out += [("epi", n - 1), ("own_dx", 0)]
    if n >= 2:
        out.append(("bwd", n - 2))
    out += [("far_part", 0), ("own_sum", 0), ("far_dx", 0), ("bwd", n - 1), ("far_sum", 0)]
    out += [("own_home", 0), ("dot", 0)]
    out += [("finish", k) for k in range(n - 2)]
    out.append(("far_home", 0))
    out += [("finish", k) for k in range(max(n - 2, 0), n)]
    out.append(("input", 0))
    return out


def per_device(tokens, norm_gain, coded, block_codes, grid, cotangent):
    n_dev = lax.axis_size("narrow")
    n_wide = lax.axis_size("wide")
    n_a = 2
    n_b = n_dev // (2 * n_a)
    me = lax.axis_index("narrow")
    core, a, b = me % 2, me // 2 % n_a, me // (2 * n_a)
    w = lax.axis_index("wide")
    rows, fcols = coded.shape
    half = fcols // 2
    ntok, d_model = tokens.shape

    def move(x, to):
        pairs = []
        for n in range(n_dev):
            c0, a0, b0 = n % 2, n // 2 % n_a, n // (2 * n_a)
            b1, a1, c1 = to(b0, a0, c0)
            pairs.append((n, (b1 % n_b * n_a + a1 % n_a) * 2 + c1 % 2))
        return lax.ppermute(x, "narrow", pairs)

    def move_wide(x, pairs):
        return lax.ppermute(x, "wide", pairs)

    def move_all(x, to):
        pairs = []
        for w0 in range(n_wide):
            for i in range(n_dev):
                goal = to(w0 // n_a, w0 % n_a, i // (2 * n_a), i // 2 % n_a, i % 2)
                if goal is not None:
                    bw1, aw1, b1, a1, c1 = goal
                    at = (bw1 * n_a + aw1) * n_dev + (b1 * n_a + a1) * 2 + c1
                    pairs.append((w0 * n_dev + i, at))
        return lax.ppermute(x, ("wide", "narrow"), pairs)

    def to_core(x):
        return move(x, lambda b0, a0, c0: (b0, a0, c0 + 1))

    def to_a(x):
        return move(x, lambda b0, a0, c0: (b0, a0 + 1, c0))

    def to_b(x, step, cross):
        return move(x, lambda b0, a0, c0: (b0 + step, a0, c0 + cross))

    onehot = (
        block_codes[:, :, None] == jnp.arange(grid.shape[0], dtype=jnp.int32)[None, None, :]
    ).astype(jnp.float32)
    scale = jnp.sum(onehot * grid[None, None, :], axis=-1) / jnp.sqrt(jnp.float32(BLOCK))
    hblk = half // BLOCK

    def my_half(x, c, width):
        return lax.dynamic_slice_in_dim(x, c * width, width, 1)

    coded_c = [my_half(coded, core, half), my_half(coded, 1 - core, half)]
    scale_c = [my_half(scale, core, hblk), my_half(scale, 1 - core, hblk)]
    parts = cuts(hblk, CHUNKS)


    last = [coded]

    def after(*xs):
        return lax.optimization_barrier((*xs, last[0]))[: len(xs)]

    def mark(x):
        last[0] = x
        return x

    weights = [None] * len(parts)

    def columns_for(x, a_to, c_to):
        out = []
        for s in range(n_b):
            for q in range(2):
                at = (((b + s) % n_b) * n_a + a_to) * 2 + (c_to + q) % 2
                out.append(lax.dynamic_slice_in_dim(x, at * rows, rows, 1))
        return jnp.concatenate(out, axis=1)

    def flip(x):
        out = []
        for s in range(n_b):
            at = 2 * s * rows
            out += [x[:, at + rows : at + 2 * rows], x[:, at : at + rows]]
        return jnp.concatenate(out, axis=1)

    def norm(x):
        x = x.astype(jnp.float32)
        inv = lax.rsqrt(jnp.mean(x * x, axis=-1, keepdims=True) + 1e-05)
        return (x * inv * norm_gain[None, :]).astype(jnp.bfloat16), inv

    part_rows = ntok // n_wide
    v = {}
    v["x"] = jnp.zeros((4 * ntok, 2 * n_b * rows), jnp.bfloat16)
    v["act"] = jnp.zeros((ntok, fcols), jnp.bfloat16)
    v["dw"] = jnp.zeros((rows, fcols), jnp.float32)
    v["dot"] = jnp.zeros((2 * ntok,), jnp.float32)
    state = [dict() for _ in parts]
    mine_at, other_at = core * half, (1 - core) * half
    b_w, a_w = w // n_a, w % n_a

    def put(x, at):
        v["x"] = lax.dynamic_update_slice(v["x"], x, (at, 0))

    def share(_):
        part = lax.dynamic_slice_in_dim(tokens, w * part_rows, part_rows, 0)
        part, _ = norm(part)
        v["share"] = to_a(mark(columns_for(part, (a + 1) % n_a, core)))

    def weight(k):
        lo, hi = parts[k]
        mine, other = after(*[coded_c[i][:, lo:hi] for i in (0, 1)])
        mine, other = [
            decode(x, scale_c[i][:, lo // BLOCK : hi // BLOCK]) for i, x in enumerate((mine, other))
        ]
        mark(other)
        mark(mine)
        got = [mine, None]
        for step in range(1, n_b):
            got.append(to_b(mine, -step, 0))
            got.append(to_b(other, -step, 1))
        got[1] = to_core(other)
        weights[k] = got

    def norm_all(_):
        (held,) = after(tokens)
        v["normed"], v["inv"] = norm(held)
        mark(v["normed"])

    def cot_swap(_):
        (held,) = after(cotangent)
        got = to_core(mark(my_half(held, 1 - core, half)))
        v["cot"] = (my_half(held, core, half), got)

    def near(_):
        (held,) = after(v["normed"])
        other = mark(columns_for(held, a, 1 - core))
        v["near"] = to_core(other)
        (v["own"],) = after(columns_for(held, a, core))

    def far(_):
        (got,) = after(v["share"])
        put(got, 2 * ntok + w * part_rows)
        mark(got)
        v["far"] = [
            (step, move_wide(got, [(i, i ^ step) for i in range(n_wide)]))
            for step in range(1, n_wide)
        ]

    def cross(_):
        got = after(*[x for _, x in v["far"]])
        for (step, _), x in zip(v["far"], got):
            put(x, 2 * ntok + (w ^ step) * part_rows)
        got = to_core(mark(flip(v["x"][2 * ntok : 3 * ntok])))
        put(v["own"], 0)
        put(v["near"], ntok)
        put(got, 3 * ntok)

    def fwd(k):
        st = state[k]
        got = after(*weights[k])
        st["w"] = jnp.concatenate(got, axis=0)
        far_pre = jnp.dot(v["x"][2 * ntok :], st["w"], preferred_element_type=jnp.float32)
        far_pre = mark(far_pre.astype(jnp.bfloat16))
        st["far_pre"] = to_a(far_pre)

    def own(k):
        st = state[k]
        (wk,) = after(st["w"])
        st["pre"] = mark(jnp.dot(v["x"][: 2 * ntok], wk, preferred_element_type=jnp.float32))

    def epi(k):
        st, (lo, hi) = state[k], parts[k]
        far_pre, pre = after(st["far_pre"], st["pre"])
        cot = jnp.concatenate([x[:, lo:hi] for x in v["cot"]], axis=0).astype(jnp.float32)
        pre = pre + far_pre.astype(jnp.float32)
        sig = jax.nn.sigmoid(pre)
        act = (pre * sig).astype(jnp.bfloat16)
        grad = (cot * sig * (1.0 + pre * (1.0 - sig))).astype(jnp.bfloat16)
        v["dot"] = v["dot"] + jnp.sum(grad.astype(jnp.float32) * pre, axis=1)
        st["grad"], st["grad_far"] = mark(grad), to_a(grad)
        v["act"] = lax.dynamic_update_slice(v["act"], act[:ntok], (0, mine_at + lo))
        st["act"] = to_core(act[ntok:])

    def both(k):
        st = state[k]
        if "both" not in st:
            st["both"] = jnp.concatenate(after(st["grad"], st["grad_far"]), axis=0)
        return st["both"]

    def bwd(k):
        st = state[k]
        (grad,) = after(both(k))
        dw = lax.dot_general(
            v["x"], grad, (((0,), (0,)), ((), ())), preferred_element_type=jnp.float32
        )
        piece = [dw[i * rows : (i + 1) * rows] for i in range(2 * n_b)]
        low = [p.astype(jnp.bfloat16) for p in piece[1:]]
        mark(low[-1])
        st["mine"], st["other"] = [piece[0]], []
        for step in range(1, n_b):
            st["mine"].append(to_b(low[2 * step - 1], step, 0))
            st["other"].append(to_b(low[2 * step], step, 1))
        st["other"].append(to_core(low[0]))

    def across(grads, ws):
        return lax.dot_general(
            jnp.concatenate(grads, axis=1), jnp.concatenate(ws, axis=1),
            (((1,), (1,)), ((), ())), preferred_element_type=jnp.float32,
        )

    def core_swap(block):
        low = mark(block[ntok:].astype(jnp.bfloat16))
        got = [to_core(low[:, (i ^ 1) * rows : ((i ^ 1) + 1) * rows]) for i in range(2 * n_b)]
        return block[:ntok], got

    def own_dx(_):
        grads = after(*[st["grad"] for st in state])
        v["own_dx"] = core_swap(across(grads, [st["w"] for st in state]))

    def far_part(_):
        if len(parts) > 1:
            grads = after(*[st["grad_far"] for st in state[:-1]])
            v["far_part"] = mark(across(grads, [st["w"] for st in state[:-1]]))

    def far_dx(_):
        (grad,) = after(state[-1]["grad_far"])
        block = across([grad], [state[-1]["w"]])
        if len(parts) > 1:
            block = block + v["far_part"]
        v["far_dx"] = core_swap(block)

    def wide_sum(block, got):
        got = after(*got)
        total = jnp.concatenate(
            [block[:, i * rows : (i + 1) * rows] + x.astype(jnp.float32) for i, x in enumerate(got)],
            axis=1,
        )
        low = mark(total.astype(jnp.bfloat16))

        def home_block(x, step):
            at = (b_w + step - b) % n_b * 2 * rows
            return lax.dynamic_slice_in_dim(x, at, 2 * rows, 1)

        part = [home_block(low, 0)]
        for step in range(1, n_b):
            pairs = [(i, (i // n_a + step) % n_b * n_a + i % n_a) for i in range(n_wide)]
            part.append(move_wide(home_block(low, step), pairs))
        return part

    def own_sum(_):
        v["own_dx"] = wide_sum(*v["own_dx"])

    def far_sum(_):
        v["far_dx"] = wide_sum(*v["far_dx"])

    def own_home(_):
        got = after(*v["own_dx"])
        v["own_part"] = mark(sum(x.astype(jnp.float32) for x in got).astype(jnp.bfloat16))
        v["own_got"] = move_all(
            v["own_part"], lambda bw, aw, b0, a0, c0: (bw, a0, b0, a0, c0) if aw != a0 else None
        )

    def far_home(_):
        got = after(*v["far_dx"])
        part = mark(sum(x.astype(jnp.float32) for x in got).astype(jnp.bfloat16))
        v["far_got"] = [
            move_all(
                part,
                lambda bw, aw, b0, a0, c0: (bw, a0, b0, 1 - a0, c0) if (aw == a0) == same else None,
            )
            for same in (True, False)
        ]

    def dot(_):
        (total,) = after(v["dot"])
        total = total[:ntok] + to_core(total[ntok:])
        step = 1
        while step < n_wide:
            total = total + move_wide(total, [(i, i ^ step) for i in range(n_wide)])
            step *= 2
        v["row_dot"] = mark(total[:, None] / (v["inv"] * d_model))

    def finish(k):
        st, (lo, hi) = state[k], parts[k]
        got = after(st["act"], *st["mine"], *st["other"])
        act, mine, other = got[0], got[1 : 1 + n_b], got[1 + n_b :]
        v["act"] = lax.dynamic_update_slice(v["act"], act, (0, other_at + lo))
        mine = sum(x.astype(jnp.float32) for x in mine)
        other = sum(x.astype(jnp.float32) for x in other)
        v["dw"] = lax.dynamic_update_slice(v["dw"], mine, (0, mine_at + lo))
        v["dw"] = lax.dynamic_update_slice(v["dw"], other, (0, other_at + lo))
        mark(mine)

    def input_grad(_):
        own_part, own_got, *far_got = after(v["own_part"], v["own_got"], *v["far_got"])
        got = jnp.where(
            a_w == a,
            own_part.astype(jnp.float32) + own_got.astype(jnp.float32),
            sum(x.astype(jnp.float32) for x in far_got),
        )
        first, second = got[:, :rows], got[:, rows:]
        normed_grad = jnp.concatenate(
            [jnp.where(core == 0, first, second), jnp.where(core == 0, second, first)], axis=1
        )
        width = d_model // n_wide
        block = lax.dynamic_slice_in_dim(tokens, w * width, width, 1).astype(jnp.float32)
        gain = lax.dynamic_slice_in_dim(norm_gain, w * width, width, 0)
        inv = v["inv"]
        v["out"] = mark(
            (inv * (normed_grad * gain[None, :]) - block * inv**3 * v["row_dot"]).astype(jnp.bfloat16)
        )

    run = {
        "share": share, "weight": weight, "norm": norm_all, "cot": cot_swap, "near": near,
        "far": far, "cross": cross, "fwd": fwd, "own": own, "epi": epi, "bwd": bwd,
        "own_dx": own_dx, "far_part": far_part, "own_sum": own_sum, "far_dx": far_dx,
        "far_sum": far_sum, "own_home": own_home, "far_home": far_home, "dot": dot,
        "finish": finish, "input": input_grad,
    }
    for name, k in plan(len(parts)):
        run[name](k)
    return (v["act"], v["dw"], v["out"])


def solution(mesh):
    placed = (
        P("narrow", None),
        P(),
        P("narrow", "wide"),
        P("narrow", "wide"),
        P(),
        P("narrow", "wide"),
    )

    return jax.shard_map(
        per_device,
        mesh=mesh,
        in_specs=placed,
        out_specs=(P("narrow", "wide"), P("narrow", "wide"), P("narrow", "wide")),
        check_vma=False,
    )
```

time: 752 us -> 554 us (0.74)
  the two profiles are of different devices: /device:TPU:0 before, /device:TPU:7 now
where the time goes in v1:
time: 554 us; the launch traced here: 544 us
  waiting for transfers between devices  337 us (61%)
  matrix products  77.7 us (14%)
  local copies, waits for them, and re-layouts  46.5 us (8%)
  starting transfers between devices  44.2 us (8%)
  other arithmetic  36.4 us (7%)
    ppermute x49, waiting for transfers between devices, move(): return lax.ppermute(x, 'narrow', pairs)  278 us
    ppermute x7, waiting for transfers between devices, move_wide(): return lax.ppermute(x, 'wide', pairs)  41.9 us
    ppermute x49, starting transfers between devices, move(): return lax.ppermute(x, 'narrow', pairs)  34.7 us
    dot_general x3, matrix products, across(): lax.dot_general(jnp.concatenate(grads, axis=1), jnp.concatenate(ws, axis=...  27.1 us
    dot_general x4, matrix products, bwd(): lax.dot_general(v['x'], grad, (((0,), (0,)), ((), ())), preferred_element...  25.6 us
    ppermute x3, waiting for transfers between devices, move_all(): return lax.ppermute(x, ('wide', 'narrow'), pairs)  17.8 us
  transfers between devices with their start and end apart: 59, of which 24 were waited for; matrix products, arithmetic and copies ran while one was open for 27% of the time, Pallas kernels for 0%

profile of v1, /device:TPU:7, one launch (start us, length us, event | category | flops | bytes accessed | tf_op | source)
XLA Modules:
  0.0 544.4 jit_solution(4668978510162568662)
XLA Ops:
  5.6 2.7 constant_dynamic-slice_fusion.3
  10.8 3.1 collective-permute-start.8
  23.3 3.6 fusion.2
  27.0 2.6 constant_dynamic-slice_fusion.18
  31.5 2.6 constant_dynamic-slice_fusion.25
  39.7 8.5 %collective-permute-done.3 = bf16[128,2048]{1,0:T(8,128)(2,1)S(1)} collective-permute-done((bf16[128,2048]{1,0:T(8,128)(2,1)}, bf16[128,2048]{1,0:T(8,128)(2,1)S(1)}, u32[]{:S(2)}, u32[]{:S(2)}) %collective-permute-start.3) | collective-permute-done | bytes 524320 | tf_op jit(solution)/shard_map/ppermute | solution.py:87
  48.5 10.3 %collective-permute-done.2 = bf16[128,2048]{1,0:T(8,128)(2,1)S(1)} collective-permute-done((bf16[128,2048]{1,0:T(8,128)(2,1)}, bf16[128,2048]{1,0:T(8,128)(2,1)S(1)}, u32[]{:S(2)}, u32[]{:S(2)}) %collective-permute-start.2) | collective-permute-done | bytes 524320 | tf_op jit(solution)/shard_map/ppermute | solution.py:87
  62.7 19.6 %collective-permute-done.7 = bf16[512,512]{1,0:T(8,128)(2,1)S(1)} collective-permute-done((bf16[512,512]{1,0:T(8,128)(2,1)S(1)}, bf16[512,512]{1,0:T(8,128)(2,1)S(1)}, u32[]{:S(2)}, u32[]{:S(2)}) %collective-permute-start.7) | collective-permute-done | bytes 524320 | tf_op jit(solution)/shard_map/ppermute | solution.py:84
  86.4 2.3 fusion.51
  90.0 2.3 collective-permute-start.15
  93.9 2.3 fusion.35
  96.3 25.4 %collective-permute-done.11 = bf16[512,384]{1,0:T(8,128)(2,1)S(1)} collective-permute-done((bf16[512,384]{1,0:T(8,128)(2,1)S(1)}, bf16[512,384]{1,0:T(8,128)(2,1)S(1)}, u32[]{:S(2)}, u32[]{:S(2)}) %collective-permute-start.11) | collective-permute-done | bytes 393248 | tf_op jit(solution)/shard_map/ppermute | solution.py:84
  122.3 7.8 %collective-permute-done.12 = bf16[512,384]{1,0:T(8,128)(2,1)S(1)} collective-permute-done((bf16[512,384]{1,0:T(8,128)(2,1)S(1)}, bf16[512,384]{1,0:T(8,128)(2,1)S(1)}, u32[]{:S(2)}, u32[]{:S(2)}) %collective-permute-start.12) | collective-permute-done | bytes 393248 | tf_op jit(solution)/shard_map/ppermute | solution.py:84
  130.4 2.3 fusion.57
  137.8 45.6 %collective-permute-done.9 = bf16[1024,512]{1,0:T(8,128)(2,1)S(1)} collective-permute-done((bf16[1024,512]{1,0:T(8,128)(2,1)S(1)}, bf16[1024,512]{1,0:T(8,128)(2,1)S(1)}, u32[]{:S(2)}, u32[]{:S(2)}) %collective-permute-start.9) | collective-permute-done | bytes 1048608 | tf_op jit(solution)/shard_map/ppermute | solution.py:84
  186.9 2.7 fusion.54
  189.6 2.3 fusion.31
  192.0 20.7 %collective-permute-done.13 = bf16[1024,384]{1,0:T(8,128)(2,1)S(1)} collective-permute-done((bf16[1024,384]{1,0:T(8,128)(2,1)S(1)}, bf16[1024,384]{1,0:T(8,128)(2,1)S(1)}, u32[]{:S(2)}, u32[]{:S(2)}) %collective-permute-start.13) | collective-permute-done | bytes 786464 | tf_op jit(solution)/shard_map/ppermute | solution.py:84
  214.1 21.1 %collective-permute-done.22 = bf16[1024,512]{1,0:T(8,128)(2,1)S(1)} collective-permute-done((bf16[1024,512]{1,0:T(8,128)(2,1)S(1)}, bf16[1024,512]{1,0:T(8,128)(2,1)S(1)}, u32[]{:S(2)}, u32[]{:S(2)}) %collective-permute-start.22) | collective-permute-done | bytes 1048608 | tf_op jit(solution)/shard_map/ppermute | solution.py:84
  235.3 4.8 fusion.115
  241.8 2.5 collective-permute-start.27
  246.9 2.3 fusion.29
  249.2 19.7 %collective-permute-done.18 = bf16[1024,512]{1,0:T(8,128)(2,1)S(1)} collective-permute-done((bf16[1024,512]{1,0:T(8,128)(2,1)S(1)}, bf16[1024,512]{1,0:T(8,128)(2,1)S(1)}, u32[]{:S(2)}, u32[]{:S(2)}) %collective-permute-start.18) | collective-permute-done | bytes 1048608 | tf_op jit(solution)/shard_map/ppermute | solution.py:84
  271.6 14.1 %collective-permute-done.24 = bf16[1024,384]{1,0:T(8,128)(2,1)S(1)} collective-permute-done((bf16[1024,384]{1,0:T(8,128)(2,1)S(1)}, bf16[1024,384]{1,0:T(8,128)(2,1)S(1)}, u32[]{:S(2)}, u32[]{:S(2)}) %collective-permute-start.24) | collective-permute-done | bytes 786464 | tf_op jit(solution)/shard_map/ppermute | solution.py:84
  285.9 6.4 %fusion.116 = (bf16[2048,384]{1,0:T(8,128)(2,1)S(1)}, f32[2048,384]{1,0:T(8,128)}) fusion(bf16[2048,2048]{1,0:T(8,128)(2,1)S(1)} %constant_dynamic-update-slice_fusion.24, bf16[2048,384]{1,0:T(8,128)(2,1)S(1)} %pad_maximum_fusion.7), kind=kOutput, calls=%fused_computation.307 | convolution fusion | flops 3222011904 | bytes 14680064 | tf_op jit(solution)/shard_map/dot_general | solution.py:256
  293.4 2.6 collective-permute-start.30
  296.0 23.1 %collective-permute-done.26 = bf16[512,512]{1,0:T(8,128)(2,1)S(1)} collective-permute-done((bf16[512,512]{1,0:T(8,128)(2,1)S(1)}, bf16[512,512]{1,0:T(8,128)(2,1)S(1)}, u32[]{:S(2)}, u32[]{:S(2)}) %collective-permute-start.26) | collective-permute-done | bytes 524320 | tf_op jit(solution)/shard_map/ppermute | solution.py:84
  321.9 2.7 collective-permute-start.23
  324.6 3.9 broadcast_in_dim.56
  329.7 6.3 %collective-permute-done.30 = bf16[512,384]{1,0:T(8,128)(2,1)S(1)} collective-permute-done((bf16[512,384]{1,0:T(8,128)(2,1)S(1)}, bf16[512,384]{1,0:T(8,128)(2,1)S(1)}, u32[]{:S(2)}, u32[]{:S(2)}) %collective-permute-start.30) | collective-permute-done | bytes 393248 | tf_op jit(solution)/shard_map/ppermute | solution.py:84
  336.0 8.4 %collective-permute-done.31 = bf16[512,384]{1,0:T(8,128)(2,1)S(1)} collective-permute-done((bf16[512,384]{1,0:T(8,128)(2,1)S(1)}, bf16[512,384]{1,0:T(8,128)(2,1)S(1)}, u32[]{:S(2)}, u32[]{:S(2)}) %collective-permute-start.31) | collective-permute-done | bytes 393248 | tf_op jit(solution)/shard_map/ppermute | solution.py:84
  347.5 8.8 %collective-permute-done.23 = bf16[1024,384]{1,0:T(8,128)(2,1)S(1)} collective-permute-done((bf16[1024,384]{1,0:T(8,128)(2,1)S(1)}, bf16[1024,384]{1,0:T(8,128)(2,1)S(1)}, u32[]{:S(2)}, u32[]{:S(2)}) %collective-permute-start.23) | collective-permute-done | bytes 786464 | tf_op jit(solution)/shard_map/ppermute | solution.py:84
  358.1 13.0 %fusion.117 = (bf16[1024,2048]{1,0:T(8,128)(2,1)}, f32[1024,2048]{1,0:T(8,128)}) fusion(bf16[2048,384]{1,0:T(8,128)(2,1)} %copy-done.10, bf16[2048,512]{1,0:T(8,128)(2,1)} %copy-done.32, bf16[2048,384]{1,0:T(8,128)(2,1)} %copy-done.33, bf16[2048,512]{1,0:T(8,128)(2,1)} %copy-done.31, bf16[1024,384]{1,0:T(8,128)(2,1)S(1)} %get-tuple-element.171, ...), kind=kOutput, calls=%fused_computation.308 | convolution fusion | flops 7562330112 | bytes 23592960 | tf_op jit(solution)/shard_map/dot_general | solution.py:269
  371.1 2.9 fusion.100
  375.1 3.8 collective-permute-done.34
  380.9 9.8 %fusion.118 = (bf16[2048,512]{1,0:T(8,128)(2,1)S(1)}, f32[2048,512]{1,0:T(8,128)}) fusion(bf16[2048,2048]{1,0:T(8,128)(2,1)} %copy-done.1, bf16[2048,512]{1,0:T(8,128)(2,1)S(1)} %pad_maximum_fusion.4), kind=kOutput, calls=%fused_computation.309 | convolution fusion | flops 4296015872 | bytes 16777216 | tf_op jit(solution)/shard_map/dot_general | solution.py:256
  392.3 9.4 %fusion.11 = f32[1024,2048]{1,0:T(8,128)S(1)} fusion(bf16[2048,512]{1,0:T(8,128)(2,1)} %copy-done.32, bf16[2048,384]{1,0:T(8,128)(2,1)} %copy-done.33, bf16[2048,512]{1,0:T(8,128)(2,1)} %copy-done.31, bf16[1024,512]{1,0:T(8,128)(2,1)} %collective-permute-done.34, bf16[1024,384]{1,0:T(8,128)(2,1)S(1)} %copy-done.16, ...), kind=kOutput, calls=%fused_computation.13 | convolution fusion | flops 5931532288 | bytes 17039360 | tf_op jit(solution)/shard_map/dot_general | solution.py:269
  406.5 4.6 fusion.119
  414.7 4.6 fusion.120
  422.9 8.3 %collective-permute-done.52 = bf16[512,1024]{1,0:T(8,128)(2,1)} collective-permute-done((bf16[512,1024]{1,0:T(8,128)(2,1)}, bf16[512,1024]{1,0:T(8,128)(2,1)}, u32[]{:S(2)}, u32[]{:S(2)}) %collective-permute-start.52) | collective-permute-done | bytes 1048608 | tf_op jit(solution)/shard_map/ppermute | solution.py:87
  440.6 13.1 %collective-permute-done.58 = f32[512]{0:T(512)S(1)} collective-permute-done((f32[512]{0:T(512)S(1)}, f32[512]{0:T(512)S(1)}, u32[]{:S(2)}, u32[]{:S(2)}) %collective-permute-start.58) | collective-permute-done | bytes 2080 | tf_op jit(solution)/shard_map/ppermute | solution.py:87
  454.7 2.6 collective-permute-start.50
  457.4 23.4 %collective-permute-done.35 = bf16[512,512]{1,0:T(8,128)(2,1)S(1)} collective-permute-done((bf16[512,512]{1,0:T(8,128)(2,1)S(1)}, bf16[512,512]{1,0:T(8,128)(2,1)S(1)}, u32[]{:S(2)}, u32[]{:S(2)}) %collective-permute-start.35) | collective-permute-done | bytes 524320 | tf_op jit(solution)/shard_map/ppermute | solution.py:84
  481.2 19.4 %collective-permute-done.36 = bf16[512,512]{1,0:T(8,128)(2,1)S(1)} collective-permute-done((bf16[512,512]{1,0:T(8,128)(2,1)S(1)}, bf16[512,512]{1,0:T(8,128)(2,1)S(1)}, u32[]{:S(2)}, u32[]{:S(2)}) %collective-permute-start.36) | collective-permute-done | bytes 524320 | tf_op jit(solution)/shard_map/ppermute | solution.py:84
  507.2 10.2 %collective-permute-done.49 = bf16[512,384]{1,0:T(8,128)(2,1)S(1)} collective-permute-done((bf16[512,384]{1,0:T(8,128)(2,1)S(1)}, bf16[512,384]{1,0:T(8,128)(2,1)S(1)}, u32[]{:S(2)}, u32[]{:S(2)}) %collective-permute-start.49) | collective-permute-done | bytes 393248 | tf_op jit(solution)/shard_map/ppermute | solution.py:84
  522.0 3.0 collective-permute-done.53
  525.0 14.7 %collective-permute-done.55 = bf16[512,1024]{1,0:T(8,128)(2,1)S(1)} collective-permute-done((bf16[512,1024]{1,0:T(8,128)(2,1)S(1)}, bf16[512,1024]{1,0:T(8,128)(2,1)S(1)}, u32[]{:S(2)}, u32[]{:S(2)}) %collective-permute-start.55) | collective-permute-done | bytes 1048608 | tf_op jit(solution)/shard_map/ppermute | solution.py:98
  541.3 2.7 fusion.50
  (325 shorter events, 102.5 us)
Async XLA Ops:
  4.0 30.0 %collective-permute-start = (bf16[128,2048]{1,0:T(8,128)(2,1)S(1)}, bf16[128,2048]{1,0:T(8,128)(2,1)}, u32[]{:S(2)}, u32[]{:S(2)}) collective-permute-start(bf16[128,2048]{1,0:T(8,128)(2,1)S(1)} %pad_maximum_fusion.9), channel_id=1, source_target_pairs={{0,2},{1,3},{2,0},{3,1},{4,6},{5,7},{6,4},{7,5},{8,10},{9,11},{10,... | collective-permute-start | bytes 1572872 | tf_op jit(solution)/shard_map/ppermute | solution.py:84
  10.8 50.0 %collective-permute-start.8 = (bf16[512,512]{1,0:T(8,128)(2,1)}, bf16[512,512]{1,0:T(8,128)(2,1)}, u32[]{:S(2)}, u32[]{:S(2)}) collective-permute-start(bf16[512,512]{1,0:T(8,128)(2,1)} %fusion.64), channel_id=1, source_target_pairs={{0,5},{1,4},{2,7},{3,6},{4,1},{5,0},{6,3},{7,2},{8,13},{9,12},{10,... | collective-permute-start | bytes 1572872 | tf_op jit(solution)/shard_map/ppermute | solution.py:84
  13.9 48.6 %collective-permute-start.6 = (bf16[512,512]{1,0:T(8,128)(2,1)}, bf16[512,512]{1,0:T(8,128)(2,1)}, u32[]{:S(2)}, u32[]{:S(2)}) collective-permute-start(bf16[512,512]{1,0:T(8,128)(2,1)} %fusion.64), channel_id=1, source_target_pairs={{0,1},{1,0},{2,3},{3,2},{4,5},{5,4},{6,7},{7,6},{8,9},{9,8},{10,11... | collective-permute-start | bytes 1572872 | tf_op jit(solution)/shard_map/ppermute | solution.py:84
  34.3 24.6 %collective-permute-start.2 = (bf16[128,2048]{1,0:T(8,128)(2,1)}, bf16[128,2048]{1,0:T(8,128)(2,1)S(1)}, u32[]{:S(2)}, u32[]{:S(2)}) collective-permute-start(bf16[128,2048]{1,0:T(8,128)(2,1)} %collective-permute-done), channel_id=1, source_target_pairs={{0,16},{8,24},{16,0},{24,8},{1,17},{9,25},{17,1},{25,9},{2,18},{10... | collective-permute-start | bytes 1572872 | tf_op jit(solution)/shard_map/ppermute | solution.py:87
  35.5 24.6 %collective-permute-start.1 = (bf16[128,2048]{1,0:T(8,128)(2,1)}, bf16[128,2048]{1,0:T(8,128)(2,1)S(1)}, u32[]{:S(2)}, u32[]{:S(2)}) collective-permute-start(bf16[128,2048]{1,0:T(8,128)(2,1)} %collective-permute-done), channel_id=1, source_target_pairs={{0,8},{8,0},{16,24},{24,16},{1,9},{9,1},{17,25},{25,17},{2,10},{10... | collective-permute-start | bytes 1572872 | tf_op jit(solution)/shard_map/ppermute | solution.py:87
  48.2 34.1 %collective-permute-start.7 = (bf16[512,512]{1,0:T(8,128)(2,1)S(1)}, bf16[512,512]{1,0:T(8,128)(2,1)S(1)}, u32[]{:S(2)}, u32[]{:S(2)}) collective-permute-start(bf16[512,512]{1,0:T(8,128)(2,1)S(1)} %copy-done.21), channel_id=1, source_target_pairs={{0,4},{1,5},{2,6},{3,7},{4,0},{5,1},{6,2},{7,3},{8,12},{9,13},{10,... | collective-permute-start | bytes 1572872 | tf_op jit(solution)/shard_map/ppermute | solution.py:84
  58.8 26.0 %collective-permute-start.4 = (bf16[512,2048]{1,0:T(8,128)(2,1)S(1)}, bf16[512,2048]{1,0:T(8,128)(2,1)S(1)}, u32[]{:S(2)}, u32[]{:S(2)}) collective-permute-start(bf16[512,2048]{1,0:T(8,128)(2,1)S(1)} %copy-done.11), channel_id=1, source_target_pairs={{0,1},{1,0},{2,3},{3,2},{4,5},{5,4},{6,7},{7,6},{8,9},{9,8},{10,11... | collective-permute-start | bytes 6291464 | tf_op jit(solution)/shard_map/ppermute | solution.py:84
  60.1 25.7 %collective-permute-start.17 = (bf16[512,1792]{1,0:T(8,128)(2,1)S(1)}, bf16[512,1792]{1,0:T(8,128)(2,1)S(1)}, u32[]{:S(2)}, u32[]{:S(2)}) collective-permute-start(bf16[512,1792]{1,0:T(8,128)(2,1)S(1)} %constant_dynamic-slice_fusion.19), channel_id=1, source_target_pairs={{0,1},{1,0},{2,3},{3,2},{4,5},{5,4},{6,7},{7,6},{8,9},{9,8},{10,11... | collective-permute-start | bytes 5505032 | tf_op jit(solution)/shard_map/ppermute | solution.py:84
  60.8 25.2 %collective-permute-start.5 = (bf16[512,2048]{1,0:T(8,128)(2,1)S(1)}, bf16[512,2048]{1,0:T(8,128)(2,1)S(1)}, u32[]{:S(2)}, u32[]{:S(2)}) collective-permute-start(bf16[512,2048]{1,0:T(8,128)(2,1)S(1)} %pad_maximum_fusion.2), channel_id=1, source_target_pairs={{0,1},{1,0},{2,3},{3,2},{4,5},{5,4},{6,7},{7,6},{8,9},{9,8},{10,11... | collective-permute-start | bytes 6291464 | tf_op jit(solution)/shard_map/ppermute | solution.py:84
  62.5 59.2 %collective-permute-start.11 = (bf16[512,384]{1,0:T(8,128)(2,1)S(1)}, bf16[512,384]{1,0:T(8,128)(2,1)S(1)}, u32[]{:S(2)}, u32[]{:S(2)}) collective-permute-start(bf16[512,384]{1,0:T(8,128)(2,1)S(1)} %fusion.67), channel_id=1, source_target_pairs={{0,4},{1,5},{2,6},{3,7},{4,0},{5,1},{6,2},{7,3},{8,12},{9,13},{10,... | collective-permute-start | bytes 1179656 | tf_op jit(solution)/shard_map/ppermute | solution.py:84
  82.3 47.8 %collective-permute-start.12 = (bf16[512,384]{1,0:T(8,128)(2,1)S(1)}, bf16[512,384]{1,0:T(8,128)(2,1)S(1)}, u32[]{:S(2)}, u32[]{:S(2)}) collective-permute-start(bf16[512,384]{1,0:T(8,128)(2,1)S(1)} %fusion.68), channel_id=1, source_target_pairs={{0,5},{1,4},{2,7},{3,6},{4,1},{5,0},{6,3},{7,2},{8,13},{9,12},{10,... | collective-permute-start | bytes 1179656 | tf_op jit(solution)/shard_map/ppermute | solution.py:84
  84.9 45.2 %collective-permute-start.10 = (bf16[512,384]{1,0:T(8,128)(2,1)S(1)}, bf16[512,384]{1,0:T(8,128)(2,1)S(1)}, u32[]{:S(2)}, u32[]{:S(2)}) collective-permute-start(bf16[512,384]{1,0:T(8,128)(2,1)S(1)} %fusion.68), channel_id=1, source_target_pairs={{0,1},{1,0},{2,3},{3,2},{4,5},{5,4},{6,7},{7,6},{8,9},{9,8},{10,11... | collective-permute-start | bytes 1179656 | tf_op jit(solution)/shard_map/ppermute | solution.py:84
  90.0 94.7 %collective-permute-start.15 = (bf16[512,512]{1,0:T(8,128)(2,1)S(1)}, bf16[512,512]{1,0:T(8,128)(2,1)S(1)}, u32[]{:S(2)}, u32[]{:S(2)}) collective-permute-start(bf16[512,512]{1,0:T(8,128)(2,1)S(1)} %fusion.65), channel_id=1, source_target_pairs={{0,4},{1,5},{2,6},{3,7},{4,0},{5,1},{6,2},{7,3},{8,12},{9,13},{10,... | collective-permute-start | bytes 1572872 | tf_op jit(solution)/shard_map/ppermute | solution.py:84
  93.5 91.8 %collective-permute-start.16 = (bf16[512,512]{1,0:T(8,128)(2,1)S(1)}, bf16[512,512]{1,0:T(8,128)(2,1)S(1)}, u32[]{:S(2)}, u32[]{:S(2)}) collective-permute-start(bf16[512,512]{1,0:T(8,128)(2,1)S(1)} %fusion.66), channel_id=1, source_target_pairs={{0,5},{1,4},{2,7},{3,6},{4,1},{5,0},{6,3},{7,2},{8,13},{9,12},{10,... | collective-permute-start | bytes 1572872 | tf_op jit(solution)/shard_map/ppermute | solution.py:84
  121.7 63.9 %collective-permute-start.14 = (bf16[512,512]{1,0:T(8,128)(2,1)S(1)}, bf16[512,512]{1,0:T(8,128)(2,1)S(1)}, u32[]{:S(2)}, u32[]{:S(2)}) collective-permute-start(bf16[512,512]{1,0:T(8,128)(2,1)S(1)} %fusion.66), channel_id=1, source_target_pairs={{0,1},{1,0},{2,3},{3,2},{4,5},{5,4},{6,7},{7,6},{8,9},{9,8},{10,11... | collective-permute-start | bytes 1572872 | tf_op jit(solution)/shard_map/ppermute | solution.py:84
  130.1 53.4 %collective-permute-start.9 = (bf16[1024,512]{1,0:T(8,128)(2,1)S(1)}, bf16[1024,512]{1,0:T(8,128)(2,1)S(1)}, u32[]{:S(2)}, u32[]{:S(2)}) collective-permute-start(bf16[1024,512]{1,0:T(8,128)(2,1)S(1)} %fusion.51), channel_id=1, source_target_pairs={{0,2},{1,3},{2,0},{3,1},{4,6},{5,7},{6,4},{7,5},{8,10},{9,11},{10,... | collective-permute-start | bytes 3145736 | tf_op jit(solution)/shard_map/ppermute | solution.py:84
  133.3 107.0 %collective-permute-start.20 = (bf16[512,384]{1,0:T(8,128)(2,1)S(1)}, bf16[512,384]{1,0:T(8,128)(2,1)S(1)}, u32[]{:S(2)}, u32[]{:S(2)}) collective-permute-start(bf16[512,384]{1,0:T(8,128)(2,1)S(1)} %fusion.69), channel_id=1, source_target_pairs={{0,4},{1,5},{2,6},{3,7},{4,0},{5,1},{6,2},{7,3},{8,12},{9,13},{10,... | collective-permute-start | bytes 1179656 | tf_op jit(solution)/shard_map/ppermute | solution.py:84
  183.5 58.2 %collective-permute-start.21 = (bf16[512,384]{1,0:T(8,128)(2,1)S(1)}, bf16[512,384]{1,0:T(8,128)(2,1)S(1)}, u32[]{:S(2)}, u32[]{:S(2)}) collective-permute-start(bf16[512,384]{1,0:T(8,128)(2,1)S(1)} %fusion.70), channel_id=1, source_target_pairs={{0,5},{1,4},{2,7},{3,6},{4,1},{5,0},{6,3},{7,2},{8,13},{9,12},{10,... | collective-permute-start | bytes 1179656 | tf_op jit(solution)/shard_map/ppermute | solution.py:84
  184.7 57.1 %collective-permute-start.19 = (bf16[512,384]{1,0:T(8,128)(2,1)S(1)}, bf16[512,384]{1,0:T(8,128)(2,1)S(1)}, u32[]{:S(2)}, u32[]{:S(2)}) collective-permute-start(bf16[512,384]{1,0:T(8,128)(2,1)S(1)} %fusion.70), channel_id=1, source_target_pairs={{0,1},{1,0},{2,3},{3,2},{4,5},{5,4},{6,7},{7,6},{8,9},{9,8},{10,11... | collective-permute-start | bytes 1179656 | tf_op jit(solution)/shard_map/ppermute | solution.py:84
  185.2 27.5 %collective-permute-start.13 = (bf16[1024,384]{1,0:T(8,128)(2,1)S(1)}, bf16[1024,384]{1,0:T(8,128)(2,1)S(1)}, u32[]{:S(2)}, u32[]{:S(2)}) collective-permute-start(bf16[1024,384]{1,0:T(8,128)(2,1)S(1)} %fusion.57), channel_id=1, source_target_pairs={{0,2},{1,3},{2,0},{3,1},{4,6},{5,7},{6,4},{7,5},{8,10},{9,11},{10,... | collective-permute-start | bytes 2359304 | tf_op jit(solution)/shard_map/ppermute | solution.py:84
  185.6 49.6 %collective-permute-start.22 = (bf16[1024,512]{1,0:T(8,128)(2,1)S(1)}, bf16[1024,512]{1,0:T(8,128)(2,1)S(1)}, u32[]{:S(2)}, u32[]{:S(2)}) collective-permute-start(bf16[1024,512]{1,0:T(8,128)(2,1)S(1)} %get-tuple-element.156), channel_id=1, source_target_pairs={{0,2},{1,3},{2,0},{3,1},{4,6},{5,7},{6,4},{7,5},{8,10},{9,11},{10,... | collective-permute-start | bytes 3145736 | tf_op jit(solution)/shard_map/ppermute | solution.py:84
  212.7 56.2 %collective-permute-start.18 = (bf16[1024,512]{1,0:T(8,128)(2,1)S(1)}, bf16[1024,512]{1,0:T(8,128)(2,1)S(1)}, u32[]{:S(2)}, u32[]{:S(2)}) collective-permute-start(bf16[1024,512]{1,0:T(8,128)(2,1)S(1)} %fusion.54), channel_id=1, source_target_pairs={{0,2},{1,3},{2,0},{3,1},{4,6},{5,7},{6,4},{7,5},{8,10},{9,11},{10,... | collective-permute-start | bytes 3145736 | tf_op jit(solution)/shard_map/ppermute | solution.py:84
  235.2 50.6 %collective-permute-start.24 = (bf16[1024,384]{1,0:T(8,128)(2,1)S(1)}, bf16[1024,384]{1,0:T(8,128)(2,1)S(1)}, u32[]{:S(2)}, u32[]{:S(2)}) collective-permute-start(bf16[1024,384]{1,0:T(8,128)(2,1)S(1)} %get-tuple-element.157), channel_id=1, source_target_pairs={{0,2},{1,3},{2,0},{3,1},{4,6},{5,7},{6,4},{7,5},{8,10},{9,11},{10,... | collective-permute-start | bytes 2359304 | tf_op jit(solution)/shard_map/ppermute | solution.py:84
  240.3 52.2 %collective-permute-start.25 = (bf16[512,512]{1,0:T(8,128)(2,1)S(1)}, bf16[512,512]{1,0:T(8,128)(2,1)S(1)}, u32[]{:S(2)}, u32[]{:S(2)}) collective-permute-start(bf16[512,512]{1,0:T(8,128)(2,1)S(1)} %get-tuple-element.287), channel_id=1, source_target_pairs={{0,1},{1,0},{2,3},{3,2},{4,5},{5,4},{6,7},{7,6},{8,9},{9,8},{10,11... | collective-permute-start | bytes 1572872 | tf_op jit(solution)/shard_map/ppermute | solution.py:84
  241.7 88.0 %collective-permute-start.29 = (bf16[512,384]{1,0:T(8,128)(2,1)S(1)}, bf16[512,384]{1,0:T(8,128)(2,1)S(1)}, u32[]{:S(2)}, u32[]{:S(2)}) collective-permute-start(bf16[512,384]{1,0:T(8,128)(2,1)S(1)} %get-tuple-element.295), channel_id=1, source_target_pairs={{0,1},{1,0},{2,3},{3,2},{4,5},{5,4},{6,7},{7,6},{8,9},{9,8},{10,11... | collective-permute-start | bytes 1179656 | tf_op jit(solution)/shard_map/ppermute | solution.py:84
  241.8 80.1 %collective-permute-start.27 = (bf16[512,512]{1,0:T(8,128)(2,1)S(1)}, bf16[512,512]{1,0:T(8,128)(2,1)S(1)}, u32[]{:S(2)}, u32[]{:S(2)}) collective-permute-start(bf16[512,512]{1,0:T(8,128)(2,1)S(1)} %get-tuple-element.274), channel_id=1, source_target_pairs={{0,5},{1,4},{2,7},{3,6},{4,1},{5,0},{6,3},{7,2},{8,13},{9,12},{10,... | collective-permute-start | bytes 1572872 | tf_op jit(solution)/shard_map/ppermute | solution.py:84
  268.9 24.5 %collective-permute-start.28 = (bf16[512,512]{1,0:T(8,128)(2,1)S(1)}, bf16[512,512]{1,0:T(8,128)(2,1)S(1)}, u32[]{:S(2)}, u32[]{:S(2)}) collective-permute-start(bf16[512,512]{1,0:T(8,128)(2,1)S(1)} %get-tuple-element.272), channel_id=1, source_target_pairs={{0,1},{1,0},{2,3},{3,2},{4,5},{5,4},{6,7},{7,6},{8,9},{9,8},{10,11... | collective-permute-start | bytes 1572872 | tf_op jit(solution)/shard_map/ppermute | solution.py:84
  285.7 33.4 %collective-permute-start.26 = (bf16[512,512]{1,0:T(8,128)(2,1)S(1)}, bf16[512,512]{1,0:T(8,128)(2,1)S(1)}, u32[]{:S(2)}, u32[]{:S(2)}) collective-permute-start(bf16[512,512]{1,0:T(8,128)(2,1)S(1)} %get-tuple-element.273), channel_id=1, source_target_pairs={{0,4},{1,5},{2,6},{3,7},{4,0},{5,1},{6,2},{7,3},{8,12},{9,13},{10,... | collective-permute-start | bytes 1572872 | tf_op jit(solution)/shard_map/ppermute | solution.py:84
  292.4 37.3 %collective-permute-start.32 = (bf16[512,384]{1,0:T(8,128)(2,1)S(1)}, bf16[512,384]{1,0:T(8,128)(2,1)S(1)}, u32[]{:S(2)}, u32[]{:S(2)}) collective-permute-start(bf16[512,384]{1,0:T(8,128)(2,1)S(1)} %get-tuple-element.282), channel_id=1, source_target_pairs={{0,1},{1,0},{2,3},{3,2},{4,5},{5,4},{6,7},{7,6},{8,9},{9,8},{10,11... | collective-permute-start | bytes 1179656 | tf_op jit(solution)/shard_map/ppermute | solution.py:84
  293.4 42.7 %collective-permute-start.30 = (bf16[512,384]{1,0:T(8,128)(2,1)S(1)}, bf16[512,384]{1,0:T(8,128)(2,1)S(1)}, u32[]{:S(2)}, u32[]{:S(2)}) collective-permute-start(bf16[512,384]{1,0:T(8,128)(2,1)S(1)} %get-tuple-element.283), channel_id=1, source_target_pairs={{0,4},{1,5},{2,6},{3,7},{4,0},{5,1},{6,2},{7,3},{8,12},{9,13},{10,... | collective-permute-start | bytes 1179656 | tf_op jit(solution)/shard_map/ppermute | solution.py:84
  319.1 25.3 %collective-permute-start.31 = (bf16[512,384]{1,0:T(8,128)(2,1)S(1)}, bf16[512,384]{1,0:T(8,128)(2,1)S(1)}, u32[]{:S(2)}, u32[]{:S(2)}) collective-permute-start(bf16[512,384]{1,0:T(8,128)(2,1)S(1)} %get-tuple-element.284), channel_id=1, source_target_pairs={{0,5},{1,4},{2,7},{3,6},{4,1},{5,0},{6,3},{7,2},{8,13},{9,12},{10,... | collective-permute-start | bytes 1179656 | tf_op jit(solution)/shard_map/ppermute | solution.py:84
  321.9 34.4 %collective-permute-start.23 = (bf16[1024,384]{1,0:T(8,128)(2,1)S(1)}, bf16[1024,384]{1,0:T(8,128)(2,1)S(1)}, u32[]{:S(2)}, u32[]{:S(2)}) collective-permute-start(bf16[1024,384]{1,0:T(8,128)(2,1)S(1)} %fusion.60), channel_id=1, source_target_pairs={{0,2},{1,3},{2,0},{3,1},{4,6},{5,7},{6,4},{7,5},{8,10},{9,11},{10,... | collective-permute-start | bytes 2359304 | tf_op jit(solution)/shard_map/ppermute | solution.py:84
  329.7 49.2 %collective-permute-start.34 = (bf16[1024,512]{1,0:T(8,128)(2,1)S(1)}, bf16[1024,512]{1,0:T(8,128)(2,1)}, u32[]{:S(2)}, u32[]{:S(2)}) collective-permute-start(bf16[1024,512]{1,0:T(8,128)(2,1)S(1)} %get-tuple-element.160), channel_id=1, source_target_pairs={{0,2},{1,3},{2,0},{3,1},{4,6},{5,7},{6,4},{7,5},{8,10},{9,11},{10,... | collective-permute-start | bytes 3145736 | tf_op jit(solution)/shard_map/ppermute | solution.py:84
  358.1 48.4 %collective-permute-start.38 = (bf16[1024,384]{1,0:T(8,128)(2,1)S(1)}, bf16[1024,384]{1,0:T(8,128)(2,1)}, u32[]{:S(2)}, u32[]{:S(2)}) collective-permute-start(bf16[1024,384]{1,0:T(8,128)(2,1)S(1)} %get-tuple-element.171), channel_id=1, source_target_pairs={{0,2},{1,3},{2,0},{3,1},{4,6},{5,7},{6,4},{7,5},{8,10},{9,11},{10,... | collective-permute-start | bytes 2359304 | tf_op jit(solution)/shard_map/ppermute | solution.py:84
  374.0 27.7 %collective-permute-start.42 = (bf16[512,512]{1,0:T(8,128)(2,1)}, bf16[512,512]{1,0:T(8,128)(2,1)S(1)}, u32[]{:S(2)}, u32[]{:S(2)}) collective-permute-start(bf16[512,512]{1,0:T(8,128)(2,1)} %get-tuple-element.235), channel_id=1, source_target_pairs={{0,1},{1,0},{2,3},{3,2},{4,5},{5,4},{6,7},{7,6},{8,9},{9,8},{10,11... | collective-permute-start | bytes 1572872 | tf_op jit(solution)/shard_map/ppermute | solution.py:84
  374.6 27.1 %collective-permute-start.41 = (bf16[512,512]{1,0:T(8,128)(2,1)}, bf16[512,512]{1,0:T(8,128)(2,1)S(1)}, u32[]{:S(2)}, u32[]{:S(2)}) collective-permute-start(bf16[512,512]{1,0:T(8,128)(2,1)} %get-tuple-element.236), channel_id=1, source_target_pairs={{0,1},{1,0},{2,3},{3,2},{4,5},{5,4},{6,7},{7,6},{8,9},{9,8},{10,11... | collective-permute-start | bytes 1572872 | tf_op jit(solution)/shard_map/ppermute | solution.py:84
  374.6 27.1 %collective-permute-start.40 = (bf16[512,512]{1,0:T(8,128)(2,1)}, bf16[512,512]{1,0:T(8,128)(2,1)}, u32[]{:S(2)}, u32[]{:S(2)}) collective-permute-start(bf16[512,512]{1,0:T(8,128)(2,1)} %get-tuple-element.237), channel_id=1, source_target_pairs={{0,1},{1,0},{2,3},{3,2},{4,5},{5,4},{6,7},{7,6},{8,9},{9,8},{10,11... | collective-permute-start | bytes 1572872 | tf_op jit(solution)/shard_map/ppermute | solution.py:84
  406.3 25.0 %collective-permute-start.52 = (bf16[512,1024]{1,0:T(8,128)(2,1)}, bf16[512,1024]{1,0:T(8,128)(2,1)}, u32[]{:S(2)}, u32[]{:S(2)}) collective-permute-start(bf16[512,1024]{1,0:T(8,128)(2,1)} %get-tuple-element.265), channel_id=1, source_target_pairs={{0,16},{8,24},{16,0},{24,8},{1,17},{9,25},{17,1},{25,9},{2,18},{10... | collective-permute-start | bytes 3145736 | tf_op jit(solution)/shard_map/ppermute | solution.py:87
  420.3 34.4 %collective-permute-start.33 = (bf16[512,512]{1,0:T(8,128)(2,1)S(1)}, bf16[512,512]{1,0:T(8,128)(2,1)S(1)}, u32[]{:S(2)}, u32[]{:S(2)}) collective-permute-start(bf16[512,512]{1,0:T(8,128)(2,1)S(1)} %copy-done.17), channel_id=1, source_target_pairs={{0,1},{1,0},{2,3},{3,2},{4,5},{5,4},{6,7},{7,6},{8,9},{9,8},{10,11... | collective-permute-start | bytes 1572872 | tf_op jit(solution)/shard_map/ppermute | solution.py:84
  422.1 32.5 %collective-permute-start.47 = (bf16[512,1024]{1,0:T(8,128)(2,1)S(1)}, bf16[512,1024]{1,0:T(8,128)(2,1)S(1)}, u32[]{:S(2)}, u32[]{:S(2)}) collective-permute-start(bf16[512,1024]{1,0:T(8,128)(2,1)S(1)} %get-tuple-element.267), channel_id=1, source_target_pairs={{0,16},{8,24},{16,0},{24,8},{1,17},{9,25},{17,1},{25,9},{2,18},{10... | collective-permute-start | bytes 3145736 | tf_op jit(solution)/shard_map/ppermute | solution.py:87
  435.3 45.5 %collective-permute-start.35 = (bf16[512,512]{1,0:T(8,128)(2,1)S(1)}, bf16[512,512]{1,0:T(8,128)(2,1)S(1)}, u32[]{:S(2)}, u32[]{:S(2)}) collective-permute-start(bf16[512,512]{1,0:T(8,128)(2,1)S(1)} %copy-done.25), channel_id=1, source_target_pairs={{0,4},{1,5},{2,6},{3,7},{4,0},{5,1},{6,2},{7,3},{8,12},{9,13},{10,... | collective-permute-start | bytes 1572872 | tf_op jit(solution)/shard_map/ppermute | solution.py:84
  453.7 46.9 %collective-permute-start.36 = (bf16[512,512]{1,0:T(8,128)(2,1)S(1)}, bf16[512,512]{1,0:T(8,128)(2,1)S(1)}, u32[]{:S(2)}, u32[]{:S(2)}) collective-permute-start(bf16[512,512]{1,0:T(8,128)(2,1)S(1)} %copy-done.24), channel_id=1, source_target_pairs={{0,5},{1,4},{2,7},{3,6},{4,1},{5,0},{6,3},{7,2},{8,13},{9,12},{10,... | collective-permute-start | bytes 1572872 | tf_op jit(solution)/shard_map/ppermute | solution.py:84
  454.6 49.3 %collective-permute-start.48 = (bf16[512,384]{1,0:T(8,128)(2,1)S(1)}, bf16[512,384]{1,0:T(8,128)(2,1)S(1)}, u32[]{:S(2)}, u32[]{:S(2)}) collective-permute-start(bf16[512,384]{1,0:T(8,128)(2,1)S(1)} %get-tuple-element.293), channel_id=1, source_target_pairs={{0,1},{1,0},{2,3},{3,2},{4,5},{5,4},{6,7},{7,6},{8,9},{9,8},{10,11... | collective-permute-start | bytes 1179656 | tf_op jit(solution)/shard_map/ppermute | solution.py:84
  454.7 62.7 %collective-permute-start.50 = (bf16[512,384]{1,0:T(8,128)(2,1)S(1)}, bf16[512,384]{1,0:T(8,128)(2,1)S(1)}, u32[]{:S(2)}, u32[]{:S(2)}) collective-permute-start(bf16[512,384]{1,0:T(8,128)(2,1)S(1)} %get-tuple-element.281), channel_id=1, source_target_pairs={{0,5},{1,4},{2,7},{3,6},{4,1},{5,0},{6,3},{7,2},{8,13},{9,12},{10,... | collective-permute-start | bytes 1179656 | tf_op jit(solution)/shard_map/ppermute | solution.py:84
  457.3 48.5 %collective-permute-start.51 = (bf16[512,384]{1,0:T(8,128)(2,1)S(1)}, bf16[512,384]{1,0:T(8,128)(2,1)S(1)}, u32[]{:S(2)}, u32[]{:S(2)}) collective-permute-start(bf16[512,384]{1,0:T(8,128)(2,1)S(1)} %get-tuple-element.279), channel_id=1, source_target_pairs={{0,1},{1,0},{2,3},{3,2},{4,5},{5,4},{6,7},{7,6},{8,9},{9,8},{10,11... | collective-permute-start | bytes 1179656 | tf_op jit(solution)/shard_map/ppermute | solution.py:84
  480.8 36.6 %collective-permute-start.49 = (bf16[512,384]{1,0:T(8,128)(2,1)S(1)}, bf16[512,384]{1,0:T(8,128)(2,1)S(1)}, u32[]{:S(2)}, u32[]{:S(2)}) collective-permute-start(bf16[512,384]{1,0:T(8,128)(2,1)S(1)} %get-tuple-element.280), channel_id=1, source_target_pairs={{0,4},{1,5},{2,6},{3,7},{4,0},{5,1},{6,2},{7,3},{8,12},{9,13},{10,... | collective-permute-start | bytes 1179656 | tf_op jit(solution)/shard_map/ppermute | solution.py:84
  503.9 35.7 %collective-permute-start.55 = (bf16[512,1024]{1,0:T(8,128)(2,1)S(1)}, bf16[512,1024]{1,0:T(8,128)(2,1)S(1)}, u32[]{:S(2)}, u32[]{:S(2)}) collective-permute-start(bf16[512,1024]{1,0:T(8,128)(2,1)S(1)} %add_convert_fusion.1), channel_id=1, source_target_pairs={{2,8},{3,9},{6,12},{7,13},{8,2},{9,3},{12,6},{13,7},{18,24},{19,25... | collective-permute-start | bytes 3145736 | tf_op jit(solution)/shard_map/ppermute | solution.py:98
  505.9 33.9 %collective-permute-start.54 = (bf16[512,1024]{1,0:T(8,128)(2,1)S(1)}, bf16[512,1024]{1,0:T(8,128)(2,1)S(1)}, u32[]{:S(2)}, u32[]{:S(2)}) collective-permute-start(bf16[512,1024]{1,0:T(8,128)(2,1)S(1)} %add_convert_fusion.1), channel_id=1, source_target_pairs={{0,2},{1,3},{4,6},{5,7},{10,8},{11,9},{14,12},{15,13},{16,18},{17,... | collective-permute-start | bytes 3145736 | tf_op jit(solution)/shard_map/ppermute | solution.py:98
  (57 other events, 605.7 us)
